TPU v7x, 32 devices: a whole 2x2x4 slice. The times are simulated.
32 devices in a mesh: section: 4 (over y, core), seq: 8 (over z, x).
Axes of the slice: x: 2, y: 2, z: 4, core: 2. Of those that a mesh axis runs over, the one named last changes fastest.
Arguments:
- queries: bfloat16 [4, 64, 4096], P('section', 'seq'), may hold values from -110 to 110
- key_value_pages: bfloat16 [4, 16, 4, 2048], P('section', 'seq'), may hold values from -5 to 5
- block_table: int32 [4, 16], replicated, may hold values from 0 to 15, as said below
- page_mask: int32 [4, 64], replicated, may hold values from 0 to 1, as said below
- noise_level: int32 [4], replicated, may hold values from 0 to 15
- level_gate: float32 [16, 4096], replicated, may hold values from 0.5 to 1.5
Outputs:
- attended: bfloat16 [4, 64, 4096], P('section', 'seq')
Inputs may be any that keep to these rules, and one draw needn't show every extreme that they name: `block_table`: each row is a permutation of 0 to 15. `page_mask`: a query span sees all pages of its own span, none of later spans, and some pages of earlier spans.
All inputs are finite; a program needn't handle non-finite values.
Results may differ from a plain program's by a relative error of at most 0.0065.
Values may be sent and summed in bfloat16 or wider, within the bound.
No kernel may reach another device: no remote copies, remote signals or barrier semaphores. Data moves between devices by JAX's collectives and lax.ppermute only.
A program may use at most 64 MiB of HBM per device.

v0:
```python
import jax
import jax.numpy as jnp
from jax import lax
from jax.sharding import PartitionSpec as P

QUERY_HEADS = 32
KEY_VALUE_HEADS = 8
HEAD_WIDTH = 128
eps = 1e-06


def body(queries, key_value_pages, block_table, page_mask, noise_level, level_gate):
    seq_count = lax.axis_size("seq")
    section_index = lax.axis_index("section")
    seq_index = lax.axis_index("seq")
    spans = page_mask.shape[0]
    pages = block_table.shape[1]
    page_length = key_value_pages.shape[2]
    span_group = QUERY_HEADS // KEY_VALUE_HEADS
    per_device = QUERY_HEADS // seq_count
    length = queries.shape[1] * seq_count
    scale = HEAD_WIDTH ** (-0.5)
    headed_queries = lax.all_to_all(queries, "seq", split_axis=2, concat_axis=1, tiled=True)
    query_rows = headed_queries.reshape(length, per_device, HEAD_WIDTH)
    onehot = (block_table[:, :, None] == jnp.arange(pages, dtype=jnp.int32)[None, None, :]).astype(
        jnp.float32
    )
    mask_row = lax.dynamic_index_in_dim(page_mask, section_index, 0, keepdims=False).reshape(
        spans, pages
    )
    visible = jnp.einsum("ci,cip->cp", mask_row.astype(jnp.float32), onehot)
    token_visible = jnp.repeat(visible, page_length, axis=1) > 0.5
    level_row = (
        jnp.arange(level_gate.shape[0], dtype=jnp.int32) == noise_level[section_index]
    ).astype(jnp.float32)
    gate_full = jnp.dot(level_row[None, :], level_gate, precision=lax.Precision.HIGHEST)[0].reshape(
        QUERY_HEADS, HEAD_WIDTH
    )
    gate_own = lax.dynamic_slice_in_dim(gate_full, seq_index * per_device, per_device, 0)

    def attend(carry, block, span):
        running, total, accum = carry
        keys = block[:, :, 0, :].reshape(length, per_device, HEAD_WIDTH)
        value_rows = block[:, :, 1, :].reshape(length, per_device, HEAD_WIDTH)
        seen = lax.dynamic_index_in_dim(token_visible, span, 0, keepdims=False)
        scores = (
            jnp.einsum("qhd,khd->qhk", query_rows, keys, preferred_element_type=jnp.float32) * scale
        )
        scores = jnp.where(seen[None, None, :], scores, -1e30)
        newmax = jnp.maximum(running, jnp.max(scores, axis=-1))
        shrink = jnp.exp(running - newmax)
        weights = jnp.where(seen[None, None, :], jnp.exp(scores - newmax[:, :, None]), 0.0)
        total = total * shrink + jnp.sum(weights, axis=-1)
        update = jnp.einsum(
            "qhk,khd->qhd",
            weights.astype(jnp.bfloat16),
            value_rows,
            preferred_element_type=jnp.float32,
        )
        accum = accum * shrink[:, :, None] + update
        return (newmax, total, accum)

    def visit(carry, block, span):
        return attend(carry, block, span)

    initial = (
        jnp.full((length, per_device), -1e30, jnp.float32),
        jnp.zeros((length, per_device), jnp.float32),
        jnp.zeros((length, per_device, HEAD_WIDTH), jnp.float32),
    )
    span_count = key_value_pages.shape[0]
    local_span_count = key_value_pages.shape[1]
    group_spread = key_value_pages.reshape(
        span_count, local_span_count, page_length, 2, KEY_VALUE_HEADS, 1, HEAD_WIDTH
    )
    group_spread = jnp.broadcast_to(
        group_spread,
        (span_count, local_span_count, page_length, 2, KEY_VALUE_HEADS, span_group, HEAD_WIDTH),
    )
    mine = lax.all_to_all(
        group_spread.reshape(
            span_count, local_span_count, page_length, 2, QUERY_HEADS * HEAD_WIDTH
        ),
        "seq",
        split_axis=4,
        concat_axis=1,
        tiled=True,
    )
    piece = lax.all_gather(mine, "section", axis=0, tiled=True)

    def inner(offset, state):
        block = lax.dynamic_index_in_dim(piece, offset, 0, keepdims=False)
        return visit(state, block, offset)

    carry = lax.fori_loop(0, piece.shape[0], inner, initial)
    running, total, accum = carry
    mixed = accum / total[:, :, None]
    normed = mixed * lax.rsqrt(jnp.mean(mixed * mixed, axis=-1, keepdims=True) + eps)
    gated = (
        (normed * gate_own[None, :, :])
        .astype(jnp.bfloat16)
        .reshape(1, length, per_device * HEAD_WIDTH)
    )
    return lax.all_to_all(gated, "seq", split_axis=1, concat_axis=2, tiled=True)


def solution(mesh):
    return jax.shard_map(
        body,
        mesh=mesh,
        in_specs=(P("section", "seq", None), P("section", "seq", None, None), P(), P(), P(), P()),
        out_specs=P("section", "seq", None),
        check_vma=False,
    )
```

profile of v0, /device:TPU:0, one launch (start us, length us, event | category | flops | bytes accessed | tf_op | source)
XLA Modules:
  0.0 108.3 jit_solution(8707232071351404596)
XLA Ops:
  0.0 4.3 %copy.54 = bf16[1,8,4096]{1,0,2:T(2,128)(2,1)S(1)} copy(bf16[1,8,4096]{2,1,0:T(8,128)(2,1)} %param.8) | data formatting | bytes 131072 | tf_op args[0]
  4.3 0.5 broadcast.64
  4.8 22.4 %reduce.4 = bf16[4096,8]{1,0:T(8,128)(2,1)S(1)} reduce(bf16[4096,1,8]{2,1,0:T(2,128)(2,1)S(1)} %bitcast.71, bf16[]{:T(256)} %broadcast.64), dimensions={1}, to_apply=%bitcast.48.reduce_sub_computation | reduce | bytes 131074
  27.2 1.7 %reshape.58 = bf16[8,2,2048]{2,1,0:T(2,128)(2,1)} reshape(bf16[4096,8]{1,0:T(8,128)(2,1)S(1)} %reduce.4) | data formatting | bytes 131072
  28.9 7.3 %all-to-all-start.1 = ((bf16[8,2,2048]{2,1,0:T(2,128)(2,1)}), bf16[8,2,2048]{2,1,0:T(2,128)(2,1)S(1)}, u32[]{:S(2)}, u32[]{:S(2)}) async-start(bf16[8,2,2048]{2,1,0:T(2,128)(2,1)} %reshape.58), calls=%async_computation.1 | async-start | bytes 131072 | tf_op jit(solution)/shard_map/all_to_all | solution.py:23
  36.2 0.7 convert_reduce_fusion
  36.9 0.1 reshape.43
  37.0 0.2 fusion.16
  37.2 0.1 broadcast_in_dim.80
  37.3 0.1 gt.12
  37.5 1.3 %copy.50 = bf16[2,4,2,8,128]{1,2,0,4,3:T(2,128)(2,1)S(1)} copy(bf16[2,4,2,8,128]{4,3,2,1,0:T(8,128)(2,1)S(1)} %broadcast_in_dim.81) | data formatting | bytes 65536 | tf_op jit(solution)/shard_map/broadcast_in_dim | solution.py:76
  38.8 0.0 copy-start.3
  38.8 5.8 %broadcast_in_dim.82 = bf16[2,4,2,8,4,128]{1,2,0,5,4,3:T(2,128)(2,1)} broadcast(bf16[2,4,2,8,128]{1,2,0,4,3:T(2,128)(2,1)S(1)} %copy.50), dimensions={0,1,2,3,5} | broadcast | bytes 163840 | tf_op jit(solution)/shard_map/broadcast_in_dim | solution.py:76
  44.6 9.3 %reshape.56 = bf16[8,2,4096]{2,1,0:T(2,128)(2,1)} reshape(bf16[4096,1,2,2,4]{4,3,2,1,0:T(2,128)(2,1)} %bitcast.68) | data formatting | bytes 262144
  53.9 0.7 dynamic_slice.27
  54.6 6.0 %all-to-all-start = ((bf16[8,2,4096]{2,1,0:T(2,128)(2,1)}), bf16[8,2,4096]{2,1,0:T(2,128)(2,1)S(1)}, u32[]{:S(2)}, u32[]{:S(2)}) async-start(bf16[8,2,4096]{2,1,0:T(2,128)(2,1)} %reshape.56), calls=%async_computation | async-start | bytes 262144 | tf_op jit(solution)/shard_map/all_to_all | solution.py:80
  60.6 0.9 fusion.13
  61.5 2.8 %reshape.59 = bf16[4096,1,8]{2,1,0:T(2,128)(2,1)S(1)} reshape(bf16[8,2,2048]{2,1,0:T(2,128)(2,1)S(1)} %all-to-all-done.1) | data formatting | bytes 131072
  64.3 1.9 %copy.55 = bf16[1,8,4096]{2,1,0:T(8,128)(2,1)S(1)} copy(bf16[1,8,4096]{1,0,2:T(2,128)(2,1)S(1)} %bitcast.72) | data formatting | bytes 131072 | tf_op jit(solution)/shard_map/all_to_all | solution.py:23
  66.3 1.6 %all-to-all-done = bf16[8,2,4096]{2,1,0:T(2,128)(2,1)S(1)} async-done(((bf16[8,2,4096]{2,1,0:T(2,128)(2,1)}), bf16[8,2,4096]{2,1,0:T(2,128)(2,1)S(1)}, u32[]{:S(2)}, u32[]{:S(2)}) %all-to-all-start) | async-done | bytes 131104 | tf_op jit(solution)/shard_map/all_to_all | solution.py:80
  67.9 10.0 %reshape.57 = bf16[4096,1,2,2,4]{4,3,2,1,0:T(2,128)(2,1)} reshape(bf16[8,2,4096]{2,1,0:T(2,128)(2,1)S(1)} %all-to-all-done) | data formatting | bytes 262144
  77.9 6.1 %copy.66 = bf16[1,2,4,2,8,512]{5,4,3,2,1,0:T(8,128)(2,1)S(1)} copy(bf16[1,2,4,2,8,512]{2,3,1,5,4,0:T(2,128)(2,1)} %bitcast.69) | data formatting | bytes 262144 | tf_op jit(solution)/shard_map/all_to_all | solution.py:80
  84.0 0.1 copy.52
  84.2 7.2 %all_gather.3 = bf16[4,16,4,2,512]{4,1,3,2,0:T(8,128)(2,1)S(1)} all-gather(bf16[1,16,4,2,512]{4,1,3,2,0:T(8,128)(2,1)S(1)} %copy.53), channel_id=1, replica_groups=mesh['section'=4,'seq'=8] {'section'}, dimensions={0}, use_global_device_ids=true | all-gather | bytes 655360 | tf_op jit(solution)/shard_map/all_gather | solution.py:89
  91.4 3.6 %while.18 = (s32[]{:T(128)}, f32[64,4]{0,1:T(4,128)S(1)}, f32[64,4]{0,1:T(4,128)S(1)}, f32[64,4,128]{2,0,1:T(8,128)S(1)}, pred[4,64]{1,0:T(4,128)(4,1)S(1)}, /*i...) while((s32[]{:T(128)}, f32[64,4]{0,1:T(4,128)S(1)}, ...), condition=%wide.region_3.4_spmd.clone, body=%wide.region_0.3_spmd.clone.sunk | while | flops 8635651 | bytes 1720753 | solution.py:95
  91.4 0.1 copy.90
  91.6 0.2 fusion.39
  91.8 0.1 fusion.40
  92.0 0.3 fusion.42
  92.3 0.1 copy.90
  92.6 0.2 fusion.39
  92.8 0.1 fusion.40
  92.9 0.3 fusion.42
  93.3 0.1 copy.90
  93.5 0.2 fusion.39
  93.7 0.1 fusion.40
  93.8 0.3 fusion.42
  94.2 0.1 copy.90
  94.4 0.2 fusion.39
  94.6 0.1 fusion.40
  94.8 0.3 fusion.42
  95.1 0.2 multiply_reduce_fusion
  95.3 0.1 multiply_convert_fusion
  95.4 0.1 copy.59
  95.5 1.0 reduce.5
  96.5 11.1 %all_to_all.51 = bf16[8,2,2048]{2,1,0:T(2,128)(2,1)S(1)} all-to-all(bf16[8,2,2048]{2,1,0:T(2,128)(2,1)S(1)} %reshape.60), channel_id=1, replica_groups=mesh['section'=4,'seq'=8] {'seq'}, dimensions={0} | all-to-all | bytes 131072 | tf_op jit(solution)/shard_map/all_to_all | solution.py:104
  107.6 0.1 reshape.61
  107.7 0.6 copy.68
  (54 shorter events, 0.9 us)
Async XLA Ops:
  0.0 60.6 %copy-start = (f32[16,4096]{1,0:T(8,128)S(1)}, f32[16,4096]{1,0:T(8,128)}, u32[]{:S(2)}) copy-start(f32[16,4096]{1,0:T(8,128)} %param.13) | copy-start | bytes 786436
  0.0 37.0 %copy-start.2 = (s32[4,16]{1,0:T(4,128)S(1)}, s32[4,16]{1,0:T(4,128)}, u32[]{:S(2)}) copy-start(s32[4,16]{1,0:T(4,128)} %param.10) | copy-start | bytes 772
  0.0 37.4 %copy-start.1 = (bf16[1,2,4,2048]{3,2,1,0:T(4,128)(2,1)S(1)}, bf16[1,2,4,2048]{3,2,1,0:T(4,128)(2,1)}, u32[]{:S(2)}) copy-start(bf16[1,2,4,2048]{3,2,1,0:T(4,128)(2,1)} %param.9) | copy-start | bytes 98308
  28.9 25.7 %all-to-all-start.1 = ((bf16[8,2,2048]{2,1,0:T(2,128)(2,1)}), bf16[8,2,2048]{2,1,0:T(2,128)(2,1)S(1)}, u32[]{:S(2)}, u32[]{:S(2)}) async-start(bf16[8,2,2048]{2,1,0:T(2,128)(2,1)} %reshape.58), calls=%async_computation.1 | async-start | bytes 131072 | tf_op jit(solution)/shard_map/all_to_all | solution.py:23
  38.8 15.2 %copy-start.3 = (s32[4]{0:T(128)S(1)}, s32[4]{0:T(128)}, u32[]{:S(2)}) copy-start(s32[4]{0:T(128)} %param.12) | copy-start | bytes 52
  54.6 13.3 %all-to-all-start = ((bf16[8,2,4096]{2,1,0:T(2,128)(2,1)}), bf16[8,2,4096]{2,1,0:T(2,128)(2,1)S(1)}, u32[]{:S(2)}, u32[]{:S(2)}) async-start(bf16[8,2,4096]{2,1,0:T(2,128)(2,1)} %reshape.56), calls=%async_computation | async-start | bytes 262144 | tf_op jit(solution)/shard_map/all_to_all | solution.py:80
where the time goes:
time: 109 us; the launch traced here: 108 us
  local copies, waits for them, and re-layouts  46.8 us (43%)
  other arithmetic  24.9 us (23%)
  blocking collectives  18.3 us (17%)
  starting transfers between devices  13.3 us (12%)
  matrix products  2.95 us (3%)
  waiting for transfers between devices  1.64 us (2%)
    unnamed x19, local copies, waits for them, and re-layouts  29.4 us
    unnamed x5, other arithmetic  23.3 us
    all_to_all x1, blocking collectives, body(): return lax.all_to_all(gated, 'seq', split_axis=1, concat_axis=2, tiled=True)  11.1 us
    all_to_all x1, starting transfers between devices, body(): lax.all_to_all(queries, 'seq', split_axis=2, concat_axis=1, tiled=True)  7.29 us
    all_gather x1, blocking collectives, body(): piece = lax.all_gather(mine, 'section', axis=0, tiled=True)  7.2 us
    broadcast_in_dim x3, local copies, waits for them, and re-layouts, body(): jnp.broadcast_to(group_spread, (span_count, local_span_count, page_length...  7.15 us
    all_to_all x3, local copies, waits for them, and re-layouts, body(): lax.all_to_all(group_spread.reshape(span_count, local_span_count, page_le...  6.26 us
    all_to_all x1, starting transfers between devices, body(): lax.all_to_all(group_spread.reshape(span_count, local_span_count, page_le...  5.98 us
  transfers between devices with their start and end apart: 2, of which 1 were waited for; matrix products, arithmetic and copies ran while one was open for 22% of the time, Pallas kernels for 0%

commit v1 on v0

--- a/solution.py
+++ b/solution.py
@@ -77,14 +77,22 @@
         group_spread,
         (span_count, local_span_count, page_length, 2, KEY_VALUE_HEADS, span_group, HEAD_WIDTH),
     )
-    mine = lax.all_to_all(
+    spans_link = lambda own_rows, mesh_ax, d0, along_dim: jnp.concatenate(
+        lax.all_to_all(
+            jnp.stack(jnp.split(own_rows, lax.axis_size(mesh_ax), axis=d0)),
+            mesh_ax,
+            concat_axis=0,
+            split_axis=0,
+        ),
+        axis=along_dim,
+    )
+    mine = spans_link(
         group_spread.reshape(
             span_count, local_span_count, page_length, 2, QUERY_HEADS * HEAD_WIDTH
         ),
-        "seq",
-        split_axis=4,
-        concat_axis=1,
-        tiled=True,
+        mesh_ax="seq",
+        d0=4,
+        along_dim=1,
     )
     piece = lax.all_gather(mine, "section", axis=0, tiled=True)
 

time: 109 us -> 81 us (0.74)
  local copies, waits for them, and re-layouts: 46.8 us -> 19.1 us
    unnamed x19 -> x24, local copies, waits for them, and re-layouts: 29.4 us -> 14.3 us
    broadcast_in_dim x3 -> x4, local copies, waits for them, and re-layouts: 7.15 us -> 0.11 us  [body(): jnp.broadcast_to(group_spread, (span_count, local_span_count, page_length...]
    all_to_all x3 -> x1, local copies, waits for them, and re-layouts: 6.26 us -> 0.11 us  [body(): lax.all_to_all(jnp.stack(jnp.split(own_rows, lax.axis_size(mesh_ax), axis...]
  transfers between devices with their start and end apart: 2 -> 2, of which waited for: 1 -> 2; matrix products, arithmetic and copies ran while one was open for 22% -> 15% of each run, Pallas kernels for 0% -> 0%
where the time goes in v1:
time: 81 us; the launch traced here: 80.5 us
  other arithmetic  24.8 us (31%)
  local copies, waits for them, and re-layouts  19.1 us (24%)
  blocking collectives  18.2 us (22%)
  starting transfers between devices  13.2 us (16%)
  matrix products  2.89 us (4%)
  waiting for transfers between devices  1.78 us (2%)
    unnamed x5, other arithmetic  23.3 us
    unnamed x24, local copies, waits for them, and re-layouts  14.3 us
    all_to_all x1, blocking collectives, body(): return lax.all_to_all(gated, 'seq', split_axis=1, concat_axis=2, tiled=True)  11 us
    all_to_all x1, starting transfers between devices, body(): lax.all_to_all(queries, 'seq', split_axis=2, concat_axis=1, tiled=True)  7.28 us
    all_gather x1, blocking collectives, body(): piece = lax.all_gather(mine, 'section', axis=0, tiled=True)  7.2 us
    all_to_all x1, starting transfers between devices, body(): lax.all_to_all(jnp.stack(jnp.split(own_rows, lax.axis_size(mesh_ax), axis...  5.91 us
    all_to_all x2, local copies, waits for them, and re-layouts, body(): lax.all_to_all(queries, 'seq', split_axis=2, concat_axis=1, tiled=True)  1.9 us
    all_to_all x1, waiting for transfers between devices, body(): lax.all_to_all(jnp.stack(jnp.split(own_rows, lax.axis_size(mesh_ax), axis...  1.7 us
  transfers between devices with their start and end apart: 2, of which 2 were waited for; matrix products, arithmetic and copies ran while one was open for 15% of the time, Pallas kernels for 0%

profile of v1, /device:TPU:0, one launch (start us, length us, event | category | flops | bytes accessed | tf_op | source)
XLA Modules:
  0.0 80.5 jit_solution(179733552045157433)
XLA Ops:
  0.0 4.3 %copy.44 = bf16[1,8,4096]{1,0,2:T(2,128)(2,1)S(1)} copy(bf16[1,8,4096]{2,1,0:T(8,128)(2,1)} %param.8) | data formatting | bytes 131072 | tf_op args[0]
  4.3 0.5 broadcast.64
  4.8 22.3 %reduce.4 = bf16[4096,8]{1,0:T(8,128)(2,1)S(1)} reduce(bf16[4096,1,8]{2,1,0:T(2,128)(2,1)S(1)} %bitcast.98, bf16[]{:T(256)} %broadcast.64), dimensions={1}, to_apply=%bitcast.77.reduce_sub_computation | reduce | bytes 131074
  27.2 1.7 %reshape.60 = bf16[8,2,2048]{2,1,0:T(2,128)(2,1)} reshape(bf16[4096,8]{1,0:T(8,128)(2,1)S(1)} %reduce.4) | data formatting | bytes 131072
  28.9 7.3 %all-to-all-start.1 = ((bf16[8,2,2048]{2,1,0:T(2,128)(2,1)}), bf16[8,2,2048]{2,1,0:T(2,128)(2,1)S(1)}, u32[]{:S(2)}, u32[]{:S(2)}) async-start(bf16[8,2,2048]{2,1,0:T(2,128)(2,1)} %reshape.60), calls=%async_computation.1 | async-start | bytes 131072 | tf_op jit(solution)/shard_map/all_to_all | solution.py:23
  36.3 0.6 constant_dynamic-update-slice_fusion.7
  36.9 0.6 constant_dynamic-update-slice_fusion.6
  37.5 0.6 constant_dynamic-update-slice_fusion.5
  38.1 0.6 constant_dynamic-update-slice_fusion.4
  38.7 0.6 constant_dynamic-update-slice_fusion.3
  39.3 0.6 constant_dynamic-update-slice_fusion.2
  39.9 0.6 constant_dynamic-update-slice_fusion.1
  40.5 0.7 convert_reduce_fusion
  41.2 0.1 reshape.47
  41.3 0.2 fusion.16
  41.5 0.1 broadcast_in_dim.80
  41.6 0.1 gt.12
  41.7 0.6 dynamic_slice.27
  42.4 0.6 constant_dynamic-update-slice_fusion
  43.0 5.9 %all-to-all-start = ((bf16[8,1,2,4,2,512]{5,3,2,4,1,0:T(4,128)(2,1)}), bf16[8,1,2,4,2,512]{5,3,2,4,1,0:T(4,128)(2,1)S(1)}, u32[]{:S(2)}, u32[]{:S(2)}) async-start(bf16[8,1,2,4,2,512]{5,3,2,4,1,0:T(4,128)(2,1)} %constant_dynamic-update-slice_fusion), calls=%async_computation | async-start | bytes 262144 | tf_op jit(solution)/shard_map/all_to_all | solution.py:81
  49.0 0.8 %fusion.13 = f32[1,32,128]{2,0,1:T(1,128)S(1)} fusion(s32[]{:T(128)} %bitcast.13, f32[16,4096]{1,0:T(8,128)S(1)} %copy-done), kind=kOutput, calls=%fused_computation.22 | convolution fusion | flops 786448 | bytes 278532 | tf_op jit(solution)/shard_map/dot_general | solution.py:36
  49.8 2.8 %reshape.61 = bf16[4096,1,8]{2,1,0:T(2,128)(2,1)S(1)} reshape(bf16[8,2,2048]{2,1,0:T(2,128)(2,1)S(1)} %all-to-all-done.1) | data formatting | bytes 131072
  52.6 1.9 %copy.45 = bf16[1,8,4096]{2,1,0:T(8,128)(2,1)S(1)} copy(bf16[1,8,4096]{1,0,2:T(2,128)(2,1)S(1)} %bitcast.99) | data formatting | bytes 131072 | tf_op jit(solution)/shard_map/all_to_all | solution.py:23
  54.6 1.7 %all-to-all-done = bf16[8,1,2,4,2,512]{5,3,2,4,1,0:T(4,128)(2,1)S(1)} async-done(((bf16[8,1,2,4,2,512]{5,3,2,4,1,0:T(4,128)(2,1)}), bf16[8,1,2,4,2,512]{5,3,2,4,1,0:T(4,128)(2,1)S(1)}, u32[]{:S(2)}, u32[]{:S(2)}) %all-to-all-start) | async-done | bytes 131104 | tf_op jit(solution)/shard_map/all_to_all | solution.py:81
  56.3 0.1 copy.42
  56.5 7.2 %all_gather.3 = bf16[4,16,4,2,512]{4,1,3,2,0:T(8,128)(2,1)S(1)} all-gather(bf16[1,16,4,2,512]{4,1,3,2,0:T(8,128)(2,1)S(1)} %copy.43), channel_id=1, replica_groups=mesh['section'=4,'seq'=8] {'section'}, dimensions={0}, use_global_device_ids=true | all-gather | bytes 655360 | tf_op jit(solution)/shard_map/all_gather | solution.py:97
  63.7 3.7 %while.18 = (s32[]{:T(128)}, f32[64,4]{0,1:T(4,128)S(1)}, f32[64,4]{0,1:T(4,128)S(1)}, f32[64,4,128]{2,0,1:T(8,128)S(1)}, pred[4,64]{1,0:T(4,128)(4,1)S(1)}, /*i...) while((s32[]{:T(128)}, f32[64,4]{0,1:T(4,128)S(1)}, ...), condition=%wide.region_3.4_spmd.clone, body=%wide.region_0.3_spmd.clone.sunk | while | flops 8635651 | bytes 1720753 | solution.py:103
  63.7 0.1 copy.79
  63.9 0.2 fusion.39
  64.1 0.1 fusion.40
  64.2 0.3 fusion.42
  64.6 0.1 copy.79
  64.8 0.2 fusion.39
  65.0 0.1 fusion.40
  65.2 0.3 fusion.42
  65.5 0.1 copy.79
  65.7 0.2 fusion.39
  65.9 0.1 fusion.40
  66.1 0.3 fusion.42
  66.5 0.1 copy.79
  66.7 0.2 fusion.39
  66.9 0.1 fusion.40
  67.0 0.3 fusion.42
  67.3 0.2 multiply_reduce_fusion
  67.5 0.1 multiply_convert_fusion
  67.8 0.9 %reduce.5 = bf16[64,512]{1,0:T(8,128)(2,1)S(1)} reduce(bf16[64,1,512]{2,1,0:T(2,128)(2,1)S(1)} %bitcast.100, bf16[]{:T(256)} %broadcast.64), dimensions={1}, to_apply=%bitcast.79.reduce_sub_computation | reduce | bytes 131074
  68.7 11.0 %all_to_all.38 = bf16[8,2,2048]{2,1,0:T(2,128)(2,1)S(1)} all-to-all(bf16[8,2,2048]{2,1,0:T(2,128)(2,1)S(1)} %reshape.62), channel_id=1, replica_groups=mesh['section'=4,'seq'=8] {'seq'}, dimensions={0} | all-to-all | bytes 131072 | tf_op jit(solution)/shard_map/all_to_all | solution.py:112
  79.8 0.6 copy.57
  (60 shorter events, 1.2 us)
Async XLA Ops:
  0.0 49.0 %copy-start = (f32[16,4096]{1,0:T(8,128)S(1)}, f32[16,4096]{1,0:T(8,128)}, u32[]{:S(2)}) copy-start(f32[16,4096]{1,0:T(8,128)} %param.13) | copy-start | bytes 786436
  4.8 31.3 %copy-start.1 = (bf16[1,2,4,2048]{3,2,1,0:T(4,128)(2,1)S(1)}, bf16[1,2,4,2048]{3,2,1,0:T(4,128)(2,1)}, u32[]{:S(2)}) copy-start(bf16[1,2,4,2048]{3,2,1,0:T(4,128)(2,1)} %param.9) | copy-start | bytes 98308
  4.8 36.5 %copy-start.2 = (s32[4,16]{1,0:T(4,128)S(1)}, s32[4,16]{1,0:T(4,128)}, u32[]{:S(2)}) copy-start(s32[4,16]{1,0:T(4,128)} %param.10) | copy-start | bytes 772
  4.8 36.9 %copy-start.3 = (s32[4]{0:T(128)S(1)}, s32[4]{0:T(128)}, u32[]{:S(2)}) copy-start(s32[4]{0:T(128)} %param.12) | copy-start | bytes 52
  28.9 14.2 %all-to-all-start.1 = ((bf16[8,2,2048]{2,1,0:T(2,128)(2,1)}), bf16[8,2,2048]{2,1,0:T(2,128)(2,1)S(1)}, u32[]{:S(2)}, u32[]{:S(2)}) async-start(bf16[8,2,2048]{2,1,0:T(2,128)(2,1)} %reshape.60), calls=%async_computation.1 | async-start | bytes 131072 | tf_op jit(solution)/shard_map/all_to_all | solution.py:23
  43.0 13.3 %all-to-all-start = ((bf16[8,1,2,4,2,512]{5,3,2,4,1,0:T(4,128)(2,1)}), bf16[8,1,2,4,2,512]{5,3,2,4,1,0:T(4,128)(2,1)S(1)}, u32[]{:S(2)}, u32[]{:S(2)}) async-start(bf16[8,1,2,4,2,512]{5,3,2,4,1,0:T(4,128)(2,1)} %constant_dynamic-update-slice_fusion), calls=%async_computation | async-start | bytes 262144 | tf_op jit(solution)/shard_map/all_to_all | solution.py:81
